TPU v7x, 32 devices: a whole 2x2x4 slice. The times are simulated.
32 devices in a mesh: ia: 4 (over y, x), ja: 4 (over z), col: 2 (over core).
Axes of the slice: x: 2, y: 2, z: 4, core: 2. Of those that a mesh axis runs over, the one named last changes fastest.
Arguments:
- pair_rep: bfloat16 [512, 512, 128], P('ia', 'ja'), may hold values from -6 to 6
- norm_gain: float32 [128], replicated, may hold values from 0.1 to 1.9
- weights: bfloat16 [4, 128, 128], P(None, None, 'col'), may hold values from -0.5 to 0.5
- residue_mask: int32 [512], replicated, may hold values 0 or 1
- product_grad: bfloat16 [512, 128, 512], P('ia', 'col', 'ja'), may hold values from -1 to 1
Outputs:
- pair_grad: bfloat16 [512, 512, 128], P('ia', 'ja')
- weight_grads: float32 [4, 128, 128], P(None, None, 'col')
All inputs are finite; a program needn't handle non-finite values.
Results may differ from a plain program's by a relative error of at most 0.0067.
Values may be sent and summed in bfloat16 or wider, within the bound.
A program may use at most 128 MiB of HBM per device.

v0:
```python
import jax
import jax.numpy as jnp
from jax import lax
from jax.sharding import PartitionSpec as P

CLIP_LIMIT = 64.0


def gate_terms(incoming, linear, gate_pre, pair_valid):
    sigmoid_gate = jax.nn.sigmoid(gate_pre)
    through = incoming * pair_valid
    return (through * sigmoid_gate, through * linear * sigmoid_gate * (1.0 - sigmoid_gate))


def on_device(pair_rep, norm_gain, weights, residue_mask, product_grad):
    row_count = pair_rep.shape[0]
    col_count = pair_rep.shape[1]
    row_first = lax.axis_index("ia") * row_count
    col_first = lax.axis_index("ja") * col_count
    validity = residue_mask.astype(jnp.float32)
    row_valid = lax.dynamic_slice_in_dim(validity, row_first, row_count)
    col_valid = lax.dynamic_slice_in_dim(validity, col_first, col_count)
    pair_valid = row_valid[:, None, None] * col_valid[None, None, :]
    floats = pair_rep.astype(jnp.float32)
    centred = floats - jnp.mean(floats, axis=-1, keepdims=True)
    inv_std = lax.rsqrt(jnp.mean(centred * centred, axis=-1, keepdims=True) + 1e-05)
    unit_rows = centred * inv_std
    normed = (unit_rows * norm_gain).astype(jnp.bfloat16)
    projected = jnp.einsum("ikd,wdc->wick", normed, weights, preferred_element_type=jnp.float32)
    left_side = (pair_valid * jax.nn.sigmoid(projected[1]) * projected[0]).astype(jnp.bfloat16)
    right_side = (pair_valid * jax.nn.sigmoid(projected[3]) * projected[2]).astype(jnp.bfloat16)
    row_panel = lax.all_gather(product_grad, "ja", axis=2, tiled=True)
    panel_part = row_panel
    grad_left = jnp.einsum(
        "icj,jck->ick",
        panel_part,
        lax.all_gather(right_side, "ia", axis=0, tiled=True),
        preferred_element_type=jnp.float32,
    )
    panel_part = row_panel
    grad_right = lax.psum_scatter(
        jnp.einsum("icj,ick->jck", panel_part, left_side, preferred_element_type=jnp.float32),
        "ia",
        scatter_dimension=0,
        tiled=True,
    )
    lin_a, gate_a = gate_terms(grad_left, projected[0], projected[1], pair_valid)
    lin_b, gate_b = gate_terms(grad_right, projected[2], projected[3], pair_valid)
    proj_grads = jnp.stack([lin_a, gate_a, lin_b, gate_b]).astype(jnp.bfloat16)
    grad_part = jnp.einsum("ikd,wick->wdc", normed, proj_grads, preferred_element_type=jnp.float32)
    input_part = jnp.einsum(
        "wick,wdc->ikd", proj_grads, weights, preferred_element_type=jnp.float32
    )
    normed_grad = lax.psum(input_part, "col")
    scaled = normed_grad * norm_gain
    pair_grad = inv_std * (
        scaled
        - jnp.mean(scaled, axis=-1, keepdims=True)
        - unit_rows * jnp.mean(scaled * unit_rows, axis=-1, keepdims=True)
    )
    summed = lax.psum(grad_part, ("ia", "ja"))
    squares = lax.psum(jnp.sum(summed * summed), "col")
    factor = jnp.minimum(1.0, CLIP_LIMIT * lax.rsqrt(squares + 1e-06))
    weight_grads = summed * factor
    return (pair_grad.astype(jnp.bfloat16), weight_grads)


def solution(mesh):
    placed = (P("ia", "ja", None), P(), P(None, None, "col"), P(), P("ia", "col", "ja"))
    return jax.shard_map(
        on_device,
        mesh=mesh,
        in_specs=placed,
        out_specs=(P("ia", "ja", None), P(None, None, "col")),
        check_vma=False,
    )
```

profile of v0, /device:TPU:0, one launch (start us, length us, event | category | flops | bytes accessed | tf_op | source)
XLA Modules:
  0.0 660.3 jit_solution(14896707460684824877)
XLA Ops:
  7.2 0.0 copy-start
  7.2 0.0 copy-start.10
  7.2 0.0 all-gather.5.cloned.1.call-start
  7.2 4.3 copy.18
  11.5 0.0 all-gather.5.cloned.1.call-update
  11.5 0.0 all-gather.3.cloned.1.call-start
  11.6 0.0 copy-done.10
  11.6 0.0 copy-start.2
  11.6 0.1 fusion.41
  11.7 0.1 broadcast_multiply_fusion.1
  11.8 0.0 copy-start.9
  11.8 3.5 convert_reduce_fusion
  15.3 0.0 copy-done.2
  15.3 4.8 fusion.10
  20.1 0.0 copy-done
  20.2 0.0 copy-done.9
  20.2 4.7 convolution_bitcast_fusion
  24.9 0.0 copy-start.1
  24.9 5.9 copy-done.1
  30.8 2.6 multiply_convert_fusion.5
  33.4 0.0 all-gather.3.cloned.1.call-update
  33.4 0.5 reduce-scatter.2.cloned.1.call-start
  33.9 129.6 %all-gather.5.cloned.1.call-done = bf16[128,64,512]{2,0,1:T(8,128)(2,1)} async-done(((bf16[128,64,128]{2,0,1:T(8,128)(2,1)}), bf16[128,64,512]{2,0,1:T(8,128)(2,1)}) %all-gather.5.cloned.1.call-update) | async-done | bytes 8388624 | tf_op jit(solution)/shard_map/all_gather | solution.py:32
  163.5 87.5 %all-gather.3.cloned.1.call-done = bf16[512,64,128]{2,1,0:T(8,128)(2,1)} async-done(((bf16[128,64,128]{2,1,0:T(8,128)(2,1)}), bf16[512,64,128]{2,1,0:T(8,128)(2,1)}) %all-gather.3.cloned.1.call-update) | async-done | bytes 8388624 | tf_op jit(solution)/shard_map/all_gather | solution.py:37
  251.0 25.2 %fusion.11 = f32[64,128,128]{2,1,0:T(8,128)} fusion(bf16[128,64,512]{2,0,1:T(8,128)(2,1)} %all-gather.5.cloned.1.call-done, bf16[512,64,128]{2,1,0:T(8,128)(2,1)} %all-gather.3.cloned.1.call-done), kind=kOutput, calls=%fused_computation.15 | convolution fusion | flops 1073741824 | bytes 20971520 | tf_op jit(solution)/shard_map/icj,jck->ick/dot_general | solution.py:34
  276.2 5.4 copy.20
  281.6 6.8 %fusion.28 = (bf16[1,128,64,128]{3,2,1,0:T(8,128)(2,1)S(1)}, bf16[1,128,64,128]{3,2,1,0:T(8,128)(2,1)}, bf16[128,64,128]{2,1,0:T(8,128)(2,1)S(1)}) fusion(f32[64,128,128]{1,0,2:T(8,128)} %copy.20, f32[128,128]{1,0:T(8,128)S(1)} %broadcast_multiply_fusion.1, f32[4,128,64,128]{3,2,0,1:T(8,128)} %copy-done.1), kind=kLoop, calls=%fused_computation.43 | loop fusion | flops 14680064 | bytes 18939904 | tf_op jit(solution)/shard_map/stack | solution.py:49
  288.5 14.1 %fusion.32 = f32[64,128,512]{2,1,0:T(8,128)} fusion(bf16[128,64,512]{2,0,1:T(8,128)(2,1)} %all-gather.5.cloned.1.call-done, bf16[128,64,128]{2,1,0:T(8,128)(2,1)S(1)} %get-tuple-element.8), kind=kOutput, calls=%fused_computation.47 | convolution fusion | flops 1073741824 | bytes 27262976 | tf_op jit(solution)/shard_map/icj,ick->jck/dot_general | solution.py:42
  302.6 16.6 %copy.23 = f32[64,128,512]{1,0,2:T(8,128)} copy(f32[64,128,512]{2,1,0:T(8,128)} %fusion.32) | data formatting | bytes 33554432 | tf_op jit(solution)/shard_map/icj,ick->jck/dot_general | solution.py:42
  319.2 0.0 reduce-scatter.2.cloned.1.call-update
  319.2 0.0 all-reduce.5.cloned.1.call-start
  319.2 153.8 %reduce-scatter.2.cloned.1.call-done = f32[128,64,128]{2,1,0:T(8,128)} async-done(((f32[512,64,128]{2,1,0:T(8,128)}), f32[128,64,128]{2,1,0:T(8,128)}) %reduce-scatter.2.cloned.1.call-update) | async-done | bytes 4194320 | tf_op jit(solution)/shard_map/reduce_scatter | solution.py:41
  473.1 0.0 copy-start.3
  473.1 0.0 copy-start.6
  473.1 6.0 fusion.30
  479.1 0.0 copy-start.7
  479.1 0.0 copy-start.8
  479.2 1.3 copy-done.7
  480.4 0.7 copy-done.8
  481.1 0.0 copy-done.3
  481.1 0.0 copy-done.6
  481.1 5.4 fusion.34
  486.5 0.0 all-reduce.5.cloned.1.call-update
  486.6 0.0 all-reduce.3.cloned.1.call-start
  486.6 6.5 convolution_bitcast_fusion.1
  493.1 0.0 all-reduce.3.cloned.1.call-update
  493.1 99.0 %all-reduce.5.cloned.1.call-done = f32[4,128,64]{1,2,0:T(8,128)} async-done(((f32[4,128,64]{1,2,0:T(8,128)}), f32[4,128,64]{1,2,0:T(8,128)}) %all-reduce.5.cloned.1.call-update) | async-done | bytes 131088 | tf_op jit(solution)/shard_map/psum | solution.py:61
  592.1 1.5 multiply_reduce_fusion.1
  593.7 3.1 psum.23
  597.4 1.6 broadcast_multiply_fusion
  599.0 32.2 %all-reduce.3.cloned.1.call-done = f32[128,128,128]{2,1,0:T(8,128)} async-done(((f32[128,128,128]{2,1,0:T(8,128)}), f32[128,128,128]{2,1,0:T(8,128)}) %all-reduce.3.cloned.1.call-update) | async-done | bytes 8388624 | tf_op jit(solution)/shard_map/psum | solution.py:54
  631.2 0.0 copy-start.4
  631.2 0.0 copy-start.5
  631.2 11.6 %multiply_reduce_fusion = (f32[128,128]{1,0:T(8,128)S(1)}, f32[128,128]{1,0:T(8,128)S(1)}) fusion(f32[128,128,128]{2,1,0:T(8,128)} %all-reduce.3.cloned.1.call-done, f32[128]{0:T(128)S(1)} %copy-done.9, f32[128,128]{1,0:T(8,128)S(1)} %add_rsqrt_fusion, f32[128,128]{1,0:T(8,128)S(1)} %broadcast_multiply_fusion.4, bf16[128,128,128]{2,1,0:T(8,128)(2,1)} %param.5), kind=kLoop, calls=%fused_computation.17 | loop fusion | flops 14647296 | bytes 12845568 | tf_op jit(solution)/shard_map/reduce_sum | solution.py:58
  642.8 0.0 copy-done.4
  642.8 0.0 copy-done.5
  642.8 10.7 %fusion.9 = bf16[128,128,128]{2,1,0:T(8,128)(2,1)} fusion(bf16[128,128,128]{2,1,0:T(8,128)(2,1)S(1)} %copy-done.4, f32[128,128,128]{2,1,0:T(8,128)S(1)} %copy-done.5, f32[128,128]{1,0:T(8,128)S(1)} %get-tuple-element.11, f32[128,128]{1,0:T(8,128)S(1)} %get-tuple-element.12, f32[128]{0:T(128)S(1)} %copy-done.9, f32[128,128]{1,0:T(8,128)S(1)} %add_rsqrt_fusion, ...), kind=kLoop, calls=%fused_computation.12 | loop fusion | flops 18874368 | bytes 17039872 | tf_op jit(solution)/shard_map/convert_element_type | solution.py:65
  (4 shorter events, 0.0 us)
Async XLA Ops:
  7.2 13.0 %copy-start = (bf16[4,128,64]{1,2,0:T(8,128)(2,1)S(1)}, bf16[4,128,64]{1,2,0:T(8,128)(2,1)}, u32[]{:S(2)}) copy-start(bf16[4,128,64]{1,2,0:T(8,128)(2,1)} %param.7) | copy-start | bytes 196612
  7.2 4.4 copy-start.10
  7.2 156.3 %all-gather.5.cloned.1.call-start = ((), (), s32[]{:S(2)}) async-start(), calls=%async_computation.2 | async-start | bytes 10485760 | tf_op jit(solution)/shard_map/all_gather | solution.py:32
  11.5 239.5 %all-gather.3.cloned.1.call-start = ((), (), s32[]{:S(2)}) async-start(), calls=%async_computation.1 | async-start | bytes 10485760 | tf_op jit(solution)/shard_map/all_gather | solution.py:37
  11.6 3.7 copy-start.2
  11.8 8.4 %copy-start.9 = (f32[128]{0:T(128)S(1)}, f32[128]{0:T(128)}, u32[]{:S(2)}) copy-start(f32[128]{0:T(128)} %param.6) | copy-start | bytes 1540
  24.9 5.9 copy-start.1
  33.4 439.6 %reduce-scatter.2.cloned.1.call-start = ((), (), s32[]{:S(2)}) async-start(), calls=%async_computation.3 | async-start | bytes 20971520 | tf_op jit(solution)/shard_map/reduce_scatter | solution.py:41
  319.2 272.9 %all-reduce.5.cloned.1.call-start = ((), (), s32[]{:S(2)}) async-start(), calls=%async_computation.5 | async-start | bytes 262144 | tf_op jit(solution)/shard_map/psum | solution.py:61
  473.1 8.0 %copy-start.3 = (bf16[128,128,128]{2,1,0:T(8,128)(2,1)S(1)}, bf16[128,128,128]{2,1,0:T(8,128)(2,1)}, u32[]{:S(2)}) copy-start(bf16[128,128,128]{2,1,0:T(8,128)(2,1)} %param.5) | copy-start | bytes 12582916
  473.1 8.0 %copy-start.6 = (bf16[1,128,64,128]{3,2,1,0:T(8,128)(2,1)S(1)}, bf16[1,128,64,128]{3,2,1,0:T(8,128)(2,1)}, u32[]{:S(2)}) copy-start(bf16[1,128,64,128]{3,2,1,0:T(8,128)(2,1)} %get-tuple-element.5) | copy-start | bytes 6291460
  479.1 1.3 copy-start.7
  479.1 2.0 copy-start.8
  486.6 144.6 %all-reduce.3.cloned.1.call-start = ((), (), s32[]{:S(2)}) async-start(), calls=%async_computation.4 | async-start | bytes 16777216 | tf_op jit(solution)/shard_map/psum | solution.py:54
  631.2 11.6 %copy-start.4 = (bf16[128,128,128]{2,1,0:T(8,128)(2,1)S(1)}, bf16[128,128,128]{2,1,0:T(8,128)(2,1)}, u32[]{:S(2)}) copy-start(bf16[128,128,128]{2,1,0:T(8,128)(2,1)} %param.5) | copy-start | bytes 12582916
  631.2 11.6 %copy-start.5 = (f32[128,128,128]{2,1,0:T(8,128)S(1)}, f32[128,128,128]{2,1,0:T(8,128)}, u32[]{:S(2)}) copy-start(f32[128,128,128]{2,1,0:T(8,128)} %all-reduce.3.cloned.1.call-done) | copy-start | bytes 25165828
Sparse Core Ops, SparseCore 0:
  11.6 151.8 all-gather.4
  165.4 85.6 all-gather.2
  319.3 153.7 reduce-scatter.1
  486.7 105.3 all-reduce.4
  594.4 36.6 all-reduce.2
where the time goes:
time: 668 us; the launch traced here: 660 us
  waiting for transfers between devices  502 us (75%)
  matrix products  55.9 us (8%)
  other arithmetic  49.3 us (7%)
  local copies, waits for them, and re-layouts  34.2 us (5%)
  between operations  14.9 us (2%)
    reduce_scatter x1, waiting for transfers between devices, on_device(): lax.psum_scatter(jnp.einsum('icj,ick->jck', panel_part, left_side, prefer...  154 us
    all_gather x1, waiting for transfers between devices, on_device(): row_panel = lax.all_gather(product_grad, 'ja', axis=2, tiled=True)  130 us
    psum x1, waiting for transfers between devices, on_device(): summed = lax.psum(grad_part, ('ia', 'ja'))  99 us
    all_gather x1, waiting for transfers between devices, on_device(): lax.all_gather(right_side, 'ia', axis=0, tiled=True)  87.5 us
    psum x1, waiting for transfers between devices, on_device(): normed_grad = lax.psum(input_part, 'col')  32.2 us
    dot_general x1, matrix products, on_device(): jnp.einsum('icj,jck->ick', panel_part, lax.all_gather(right_side, 'ia', a...  25.2 us
    dot_general x1, local copies, waits for them, and re-layouts, on_device(): jnp.einsum('icj,ick->jck', panel_part, left_side, preferred_element_type=...  16.6 us
    dot_general x1, matrix products, on_device(): jnp.einsum('icj,ick->jck', panel_part, left_side, preferred_element_type=...  14.1 us
  transfers between devices with their start and end apart: 5, of which 5 were waited for; matrix products, arithmetic and copies ran while one was open for 4% of the time, Pallas kernels for 0%

commit v1 on v0

--- a/solution.py
+++ b/solution.py
@@ -4,6 +4,16 @@
 from jax.sharding import PartitionSpec as P
 
 CLIP_LIMIT = 64.0
+
+
+def gather_by_hops(shard, axis, dim):
+    n_dev = lax.axis_size(axis)
+    held, blocks = (shard, [shard])
+    for _ in range(n_dev - 1):
+        held = lax.ppermute(held, axis, [(i, (i + 1) % n_dev) for i in range(n_dev)])
+        blocks.insert(0, held)
+    flat = jnp.concatenate(blocks, axis=dim)
+    return jnp.roll(flat, (lax.axis_index(axis) + 1) * shard.shape[dim], axis=dim)
 
 
 def gate_terms(incoming, linear, gate_pre, pair_valid):
@@ -29,7 +39,7 @@
     projected = jnp.einsum("ikd,wdc->wick", normed, weights, preferred_element_type=jnp.float32)
     left_side = (pair_valid * jax.nn.sigmoid(projected[1]) * projected[0]).astype(jnp.bfloat16)
     right_side = (pair_valid * jax.nn.sigmoid(projected[3]) * projected[2]).astype(jnp.bfloat16)
-    row_panel = lax.all_gather(product_grad, "ja", axis=2, tiled=True)
+    row_panel = gather_by_hops(product_grad, "ja", 2)
     panel_part = row_panel
     grad_left = jnp.einsum(
         "icj,jck->ick",

time: 668 us -> 619 us (0.927)
  waiting for transfers between devices: 502 us -> 427 us
  local copies, waits for them, and re-layouts: 34.2 us -> 54.9 us
    ppermute x0 -> x3, waiting for transfers between devices: none -> 144 us  [gather_by_hops(): lax.ppermute(held, axis, [(i, (i + 1) % n_dev) for i in range(n_dev)])]
    all_gather x1 -> x0, waiting for transfers between devices: 130 us -> none  [on_device(): row_panel = lax.all_gather(product_grad, 'ja', axis=2, tiled=True)]
    all_gather x1, waiting for transfers between devices: 87.5 us -> 0.01 us  [on_device(): lax.all_gather(right_side, 'ia', axis=0, tiled=True)]
    unnamed x23 -> x36, local copies, waits for them, and re-layouts: 12.2 us -> 29.9 us
  transfers between devices with their start and end apart: 5 -> 7, of which waited for: 5 -> 6; matrix products, arithmetic and copies ran while one was open for 4% -> 5% of each run, Pallas kernels for 0% -> 0%
where the time goes in v1:
time: 619 us; the launch traced here: 613 us
  waiting for transfers between devices  427 us (69%)
  matrix products  60 us (10%)
  local copies, waits for them, and re-layouts  54.9 us (9%)
  other arithmetic  49.6 us (8%)
  between operations  15 us (2%)
    reduce_scatter x1, waiting for transfers between devices, on_device(): lax.psum_scatter(jnp.einsum('icj,ick->jck', panel_part, left_side, prefer...  152 us
    ppermute x3, waiting for transfers between devices, gather_by_hops(): lax.ppermute(held, axis, [(i, (i + 1) % n_dev) for i in range(n_dev)])  144 us
    psum x1, waiting for transfers between devices, on_device(): summed = lax.psum(grad_part, ('ia', 'ja'))  98.9 us
    psum x1, waiting for transfers between devices, on_device(): normed_grad = lax.psum(input_part, 'col')  32.2 us
    unnamed x36, local copies, waits for them, and re-layouts  29.9 us
    dot_general x1, matrix products, on_device(): jnp.einsum('icj,jck->ick', panel_part, lax.all_gather(right_side, 'ia', a...  25.2 us
    dot_general x1, local copies, waits for them, and re-layouts, on_device(): jnp.einsum('icj,ick->jck', panel_part, left_side, preferred_element_type=...  16.6 us
    dot_general x1, matrix products, on_device(): jnp.einsum('icj,ick->jck', panel_part, left_side, preferred_element_type=...  14.2 us
  transfers between devices with their start and end apart: 7, of which 6 were waited for; matrix products, arithmetic and copies ran while one was open for 5% of the time, Pallas kernels for 0%

profile of v1, /device:TPU:0, one launch (start us, length us, event | category | flops | bytes accessed | tf_op | source)
XLA Modules:
  0.0 613.5 jit_solution(15077956494862034796)
XLA Ops:
  7.2 0.0 copy-start
  7.2 0.0 all-gather.2.cloned.1.call-start
  7.2 0.0 copy-start.2
  7.2 0.0 copy-start.13
  7.3 0.0 copy-start.12
  7.3 3.5 convert_reduce_fusion
  10.8 0.0 copy-done.2
  10.8 4.8 fusion.10
  15.6 0.0 copy-done.13
  15.6 0.1 fusion.45
  15.7 0.1 broadcast_multiply_fusion.1
  15.8 0.0 copy-done
  15.8 0.0 copy-done.12
  15.8 8.7 %convolution_bitcast_fusion = f32[4,128,64,128]{3,2,0,1:T(8,128)S(1)} fusion(bf16[128,128,128]{2,1,0:T(8,128)(2,1)} %param.5, f32[128]{0:T(128)S(1)} %copy-done.12, f32[128,128]{1,0:T(8,128)S(1)} %add_rsqrt_fusion, f32[128,128]{1,0:T(8,128)S(1)} %broadcast_multiply_fusion.4, bf16[4,128,64]{1,2,0:T(8,128)(2,1)S(1)} %copy-done), kind=kOutput, calls=%fused_computation.7 | convolution fusion | flops 1084227584 | bytes 21168640 | tf_op jit(solution)/shard_map/ikd,wdc->wick/dot_general | solution.py:39
  24.5 0.0 copy-start.1
  24.6 5.7 copy-done.1
  30.3 2.6 multiply_convert_fusion.5
  32.9 0.0 all-gather.2.cloned.1.call-update
  32.9 0.0 reduce-scatter.2.cloned.1.call-start
  33.0 0.0 copy-done.6
  33.0 1.4 copy.20
  34.3 3.1 collective-permute-start
  37.4 47.6 %collective-permute-done = bf16[128,64,128]{2,0,1:T(8,128)(2,1)S(1)} collective-permute-done((bf16[128,64,128]{2,0,1:T(8,128)(2,1)S(1)}, bf16[128,64,128]{2,0,1:T(8,128)(2,1)S(1)}, u32[]{:S(2)}, u32[]{:S(2)}) %collective-permute-start) | collective-permute-done | bytes 2097184 | tf_op jit(solution)/shard_map/ppermute | solution.py:13
  85.1 1.3 copy-done.7
  86.4 0.0 collective-permute-start.1
  86.4 48.7 %collective-permute-done.1 = bf16[128,64,128]{2,0,1:T(8,128)(2,1)} collective-permute-done((bf16[128,64,128]{2,0,1:T(8,128)(2,1)S(1)}, bf16[128,64,128]{2,0,1:T(8,128)(2,1)}, u32[]{:S(2)}, u32[]{:S(2)}) %collective-permute-start.1) | collective-permute-done | bytes 2097184 | tf_op jit(solution)/shard_map/ppermute | solution.py:13
  135.1 0.5 collective-permute-start.2
  135.6 0.0 copy-start.8
  135.6 48.0 %collective-permute-done.2 = bf16[128,64,128]{2,0,1:T(8,128)(2,1)} collective-permute-done((bf16[128,64,128]{2,0,1:T(8,128)(2,1)}, bf16[128,64,128]{2,0,1:T(8,128)(2,1)}, u32[]{:S(2)}, u32[]{:S(2)}) %collective-permute-start.2) | collective-permute-done | bytes 2097184 | tf_op jit(solution)/shard_map/ppermute | solution.py:13
  183.6 3.4 constant_dynamic-update-slice_fusion.7
  187.0 3.3 constant_dynamic-update-slice_fusion.6
  190.2 0.0 copy-done.8
  190.2 1.6 constant_dynamic-update-slice_fusion.5
  191.8 2.9 constant_dynamic-update-slice_fusion.4
  194.7 3.3 constant_dynamic-update-slice_fusion.3
  198.1 3.4 constant_dynamic-update-slice_fusion.2
  201.5 1.6 constant_dynamic-update-slice_fusion.1
  203.1 2.8 constant_dynamic-update-slice_fusion
  205.9 25.2 %fusion.11 = f32[64,128,128]{2,1,0:T(8,128)} fusion(bf16[512,64,128]{2,1,0:T(8,128)(2,1)} %all-gather.2.cloned.1.call-done, bf16[128,64,1024]{2,0,1:T(8,128)(2,1)} %constant_dynamic-update-slice_fusion, s32[]{:T(128)S(6)} %select_n.22), kind=kOutput, calls=%fused_computation.15 | convolution fusion | flops 1073741824 | bytes 20971524 | tf_op jit(solution)/shard_map/icj,jck->ick/dot_general | solution.py:44
  231.1 5.6 copy.24
  236.7 7.0 %fusion.31 = (bf16[1,128,64,128]{3,2,1,0:T(8,128)(2,1)S(1)}, bf16[1,128,64,128]{3,2,1,0:T(8,128)(2,1)}, bf16[128,64,128]{2,1,0:T(8,128)(2,1)S(1)}) fusion(f32[64,128,128]{1,0,2:T(8,128)} %copy.24, f32[128,128]{1,0:T(8,128)S(1)} %broadcast_multiply_fusion.1, f32[4,128,64,128]{3,2,0,1:T(8,128)} %copy-done.1), kind=kLoop, calls=%fused_computation.46 | loop fusion | flops 14680064 | bytes 18939904 | tf_op jit(solution)/shard_map/stack | solution.py:59
  243.7 14.2 %fusion.13 = f32[64,128,512]{2,1,0:T(8,128)} fusion(bf16[128,64,1024]{2,0,1:T(8,128)(2,1)} %constant_dynamic-update-slice_fusion, s32[]{:T(128)S(6)} %select_n.22, bf16[128,64,128]{2,1,0:T(8,128)(2,1)S(1)} %get-tuple-element.8), kind=kOutput, calls=%fused_computation.18 | convolution fusion | flops 1073741824 | bytes 27262980 | tf_op jit(solution)/shard_map/icj,ick->jck/dot_general | solution.py:52
  257.9 16.6 %copy.27 = f32[64,128,512]{1,0,2:T(8,128)} copy(f32[64,128,512]{2,1,0:T(8,128)} %fusion.13) | data formatting | bytes 33554432 | tf_op jit(solution)/shard_map/icj,ick->jck/dot_general | solution.py:52
  274.4 0.0 reduce-scatter.2.cloned.1.call-update
  274.4 0.0 all-reduce.5.cloned.1.call-start
  274.5 151.6 %reduce-scatter.2.cloned.1.call-done = f32[128,64,128]{2,1,0:T(8,128)} async-done(((f32[512,64,128]{2,1,0:T(8,128)}), f32[128,64,128]{2,1,0:T(8,128)}) %reduce-scatter.2.cloned.1.call-update) | async-done | bytes 4194320 | tf_op jit(solution)/shard_map/reduce_scatter | solution.py:51
  426.1 6.1 fusion.33
  432.2 0.0 copy-start.10
  432.2 0.0 copy-start.11
  432.2 1.3 copy-done.10
  433.6 0.6 copy-done.11
  434.2 0.0 copy-done.3
  434.2 5.4 fusion.36
  439.6 0.0 all-reduce.5.cloned.1.call-update
  439.7 0.0 all-reduce.3.cloned.1.call-start
  439.7 6.5 %convolution_bitcast_fusion.1 = f32[128,128,128]{2,1,0:T(8,128)} fusion(bf16[1,128,64,128]{3,2,1,0:T(8,128)(2,1)} %copy-done.11, bf16[1,128,64,128]{3,2,1,0:T(8,128)(2,1)} %copy-done.10, bf16[1,128,64,128]{3,2,1,0:T(8,128)(2,1)} %get-tuple-element.5, bf16[1,128,64,128]{3,2,1,0:T(8,128)(2,1)S(1)} %get-tuple-element.4, bf16[4,128,64]{1,2,0:T(8,128)(2,1)S(1)} %copy-done), kind=kOutput, calls=%fused_computation.45 | convolution fusion | flops 1086324736 | bytes 16842752 | tf_op jit(solution)/shard_map/wick,wdc->ikd/dot_general | solution.py:61
  446.2 0.0 all-reduce.3.cloned.1.call-update
  446.3 98.9 %all-reduce.5.cloned.1.call-done = f32[4,128,64]{1,2,0:T(8,128)} async-done(((f32[4,128,64]{1,2,0:T(8,128)}), f32[4,128,64]{1,2,0:T(8,128)}) %all-reduce.5.cloned.1.call-update) | async-done | bytes 131088 | tf_op jit(solution)/shard_map/psum | solution.py:71
  545.2 1.5 multiply_reduce_fusion.1
  546.8 3.1 psum.23
  550.5 1.6 broadcast_multiply_fusion
  552.1 32.2 %all-reduce.3.cloned.1.call-done = f32[128,128,128]{2,1,0:T(8,128)} async-done(((f32[128,128,128]{2,1,0:T(8,128)}), f32[128,128,128]{2,1,0:T(8,128)}) %all-reduce.3.cloned.1.call-update) | async-done | bytes 8388624 | tf_op jit(solution)/shard_map/psum | solution.py:64
  584.3 11.6 %multiply_reduce_fusion = (f32[128,128]{1,0:T(8,128)S(1)}, f32[128,128]{1,0:T(8,128)S(1)}) fusion(f32[128,128,128]{2,1,0:T(8,128)} %all-reduce.3.cloned.1.call-done, f32[128]{0:T(128)S(1)} %copy-done.12, f32[128,128]{1,0:T(8,128)S(1)} %add_rsqrt_fusion, f32[128,128]{1,0:T(8,128)S(1)} %broadcast_multiply_fusion.4, bf16[128,128,128]{2,1,0:T(8,128)(2,1)} %param.5), kind=kLoop, calls=%fused_computation.17 | loop fusion | flops 14647296 | bytes 12845568 | tf_op jit(solution)/shard_map/reduce_sum | solution.py:68
  595.9 10.7 %fusion.9 = bf16[128,128,128]{2,1,0:T(8,128)(2,1)} fusion(bf16[128,128,128]{2,1,0:T(8,128)(2,1)S(1)} %copy-done.4, f32[128,128,128]{2,1,0:T(8,128)S(1)} %copy-done.5, f32[128,128]{1,0:T(8,128)S(1)} %get-tuple-element.11, f32[128,128]{1,0:T(8,128)S(1)} %get-tuple-element.12, f32[128]{0:T(128)S(1)} %copy-done.12, f32[128,128]{1,0:T(8,128)S(1)} %add_rsqrt_fusion, ...), kind=kLoop, calls=%fused_computation.12 | loop fusion | flops 18874368 | bytes 17039872 | tf_op jit(solution)/shard_map/convert_element_type | solution.py:75
  (14 shorter events, 0.1 us)
Async XLA Ops:
  7.2 8.6 %copy-start = (bf16[4,128,64]{1,2,0:T(8,128)(2,1)S(1)}, bf16[4,128,64]{1,2,0:T(8,128)(2,1)}, u32[]{:S(2)}) copy-start(bf16[4,128,64]{1,2,0:T(8,128)(2,1)} %param.7) | copy-start | bytes 196612
  7.2 198.7 %all-gather.2.cloned.1.call-start = ((), (), s32[]{:S(2)}) async-start(), calls=%async_computation.1 | async-start | bytes 10485760 | tf_op jit(solution)/shard_map/all_gather | solution.py:47
  7.2 3.6 copy-start.2
  7.2 8.4 %copy-start.13 = (s32[512]{0:T(512)S(1)}, s32[512]{0:T(512)}, u32[]{:S(2)}) copy-start(s32[512]{0:T(512)} %param.8) | copy-start | bytes 6148
  7.3 8.6 %copy-start.12 = (f32[128]{0:T(128)S(1)}, f32[128]{0:T(128)}, u32[]{:S(2)}) copy-start(f32[128]{0:T(128)} %param.6) | copy-start | bytes 1540
  24.5 5.7 copy-start.1
  30.3 2.7 copy-start.6
  32.9 393.2 %reduce-scatter.2.cloned.1.call-start = ((), (), s32[]{:S(2)}) async-start(), calls=%async_computation.2 | async-start | bytes 20971520 | tf_op jit(solution)/shard_map/reduce_scatter | solution.py:51
  34.3 50.8 %collective-permute-start = (bf16[128,64,128]{2,0,1:T(8,128)(2,1)S(1)}, bf16[128,64,128]{2,0,1:T(8,128)(2,1)S(1)}, u32[]{:S(2)}, u32[]{:S(2)}) collective-permute-start(bf16[128,64,128]{2,0,1:T(8,128)(2,1)S(1)} %copy.20), channel_id=1, source_target_pairs={{0,2},{2,4},{4,6},{6,0},{1,3},{3,5},{5,7},{7,1},{8,10},{10,12},{12... | collective-permute-start | bytes 6291464 | tf_op jit(solution)/shard_map/ppermute | solution.py:13
  85.1 1.3 copy-start.7
  86.4 48.7 %collective-permute-start.1 = (bf16[128,64,128]{2,0,1:T(8,128)(2,1)S(1)}, bf16[128,64,128]{2,0,1:T(8,128)(2,1)}, u32[]{:S(2)}, u32[]{:S(2)}) collective-permute-start(bf16[128,64,128]{2,0,1:T(8,128)(2,1)S(1)} %collective-permute-done), channel_id=1, source_target_pairs={{0,2},{2,4},{4,6},{6,0},{1,3},{3,5},{5,7},{7,1},{8,10},{10,12},{12... | collective-permute-start | bytes 6291464 | tf_op jit(solution)/shard_map/ppermute | solution.py:13
  135.1 48.5 %collective-permute-start.2 = (bf16[128,64,128]{2,0,1:T(8,128)(2,1)}, bf16[128,64,128]{2,0,1:T(8,128)(2,1)}, u32[]{:S(2)}, u32[]{:S(2)}) collective-permute-start(bf16[128,64,128]{2,0,1:T(8,128)(2,1)} %collective-permute-done.1), channel_id=1, source_target_pairs={{0,2},{2,4},{4,6},{6,0},{1,3},{3,5},{5,7},{7,1},{8,10},{10,12},{12... | collective-permute-start | bytes 6291464 | tf_op jit(solution)/shard_map/ppermute | solution.py:13
  135.6 54.7 %copy-start.8 = (bf16[128,64,128]{2,0,1:T(8,128)(2,1)S(1)}, bf16[128,64,128]{2,0,1:T(8,128)(2,1)}, u32[]{:S(2)}) copy-start(bf16[128,64,128]{2,0,1:T(8,128)(2,1)} %copy-done.7) | copy-start | bytes 6291460
  274.4 270.8 %all-reduce.5.cloned.1.call-start = ((), (), s32[]{:S(2)}) async-start(), calls=%async_computation.4 | async-start | bytes 262144 | tf_op jit(solution)/shard_map/psum | solution.py:71
  426.1 8.1 %copy-start.3 = (bf16[128,128,128]{2,1,0:T(8,128)(2,1)S(1)}, bf16[128,128,128]{2,1,0:T(8,128)(2,1)}, u32[]{:S(2)}) copy-start(bf16[128,128,128]{2,1,0:T(8,128)(2,1)} %param.5) | copy-start | bytes 12582916
  426.1 8.1 %copy-start.9 = (bf16[1,128,64,128]{3,2,1,0:T(8,128)(2,1)S(1)}, bf16[1,128,64,128]{3,2,1,0:T(8,128)(2,1)}, u32[]{:S(2)}) copy-start(bf16[1,128,64,128]{3,2,1,0:T(8,128)(2,1)} %get-tuple-element.5) | copy-start | bytes 6291460
  432.2 1.3 copy-start.10
  432.2 2.0 copy-start.11
  439.7 144.6 %all-reduce.3.cloned.1.call-start = ((), (), s32[]{:S(2)}) async-start(), calls=%async_computation.3 | async-start | bytes 16777216 | tf_op jit(solution)/shard_map/psum | solution.py:64
  584.3 11.6 %copy-start.4 = (bf16[128,128,128]{2,1,0:T(8,128)(2,1)S(1)}, bf16[128,128,128]{2,1,0:T(8,128)(2,1)}, u32[]{:S(2)}) copy-start(bf16[128,128,128]{2,1,0:T(8,128)(2,1)} %param.5) | copy-start | bytes 12582916
  584.3 11.6 %copy-start.5 = (f32[128,128,128]{2,1,0:T(8,128)S(1)}, f32[128,128,128]{2,1,0:T(8,128)}, u32[]{:S(2)}) copy-start(f32[128,128,128]{2,1,0:T(8,128)} %all-reduce.3.cloned.1.call-done) | copy-start | bytes 25165828
Sparse Core Ops, SparseCore 0:
  33.0 90.1 all-gather.1
  274.6 151.5 reduce-scatter.1
  439.8 105.3 all-reduce.4
  547.5 36.6 all-reduce.2
